TPU v7x, 32 devices: a whole 2x2x4 slice. The times are simulated.
32 devices in a mesh: gy: 4 (over x, core), gx: 8 (over z, y).
Axes of the slice: x: 2, y: 2, z: 4, core: 2. Of those that a mesh axis runs over, the one named last changes fastest.
Arguments:
- first_factor: bfloat16 [4096, 2048], P('gy', 'gx'), may hold values from -6 to 6
- second_factor: bfloat16 [2048, 8192], P('gy', 'gx'), may hold values from -0.125 to 0.125
- result_in: float32 [4096, 8192], P('gy', 'gx'), may hold values from -6 to 6
- pivot_scale: float32 [2048], replicated, may hold values from 0.25 to 1.75
Outputs:
- corrected: float32 [4096, 8192], P('gy', 'gx')
All inputs are finite; a program needn't handle non-finite values.
Results may differ from a plain program's by a relative error of at most 0.002.
Values may be sent and summed in bfloat16 or wider, within the bound.
A program may use at most 128 MiB of HBM per device.

v0:
```python
import jax
import jax.numpy as jnp
from jax import lax
from jax.sharding import PartitionSpec as P


def join_panel(left_panel, right_panel):
    return jnp.dot(left_panel, right_panel, preferred_element_type=jnp.float32)


def shards(first_factor, second_factor, result_in, pivot_scale):
    share = first_factor.shape[1]
    part_scale = lax.dynamic_slice_in_dim(pivot_scale, lax.axis_index("gx") * share, share)
    scaled_left = (first_factor.astype(jnp.float32) * part_scale).astype(jnp.bfloat16)
    left_line = lax.all_gather(scaled_left, "gx", axis=1, tiled=True)
    total = join_panel(left_line, lax.all_gather(second_factor, "gy", axis=0, tiled=True))
    corrected = result_in - total
    row_power = lax.psum(jnp.sum(corrected * corrected, axis=1), "gx")
    corrected = (
        corrected
        * lax.rsqrt(row_power / (corrected.shape[1] * lax.axis_size("gx")) + 1e-06)[:, None]
    )
    return corrected


def solution(mesh):
    return jax.shard_map(
        shards,
        mesh=mesh,
        in_specs=(P("gy", "gx"), P("gy", "gx"), P("gy", "gx"), P()),
        out_specs=P("gy", "gx"),
        check_vma=False,
    )
```

profile of v0, /device:TPU:0, one launch (start us, length us, event | category | flops | bytes accessed | tf_op | source)
XLA Modules:
  0.0 169.9 jit_solution(15891152812098854044)
XLA Ops:
  6.5 0.0 all-gather.5.cloned.1.call-start
  6.5 0.7 all-gather.5.cloned.1.call-update
  7.3 0.0 all-gather.3.cloned.1.call-start
  7.3 0.8 dynamic_slice.3
  8.1 2.0 %multiply_convert_fusion = bf16[1024,256]{1,0:T(8,128)(2,1)} fusion(bf16[1024,256]{1,0:T(8,128)(2,1)} %param.4, f32[256]{0:T(256)S(1)} %dynamic_slice.3), kind=kLoop, calls=%fused_computation.3 | loop fusion | flops 786432 | bytes 1049600 | tf_op jit(solution)/shard_map/convert_element_type | solution.py:14
  10.1 0.0 all-gather.3.cloned.1.call-update
  10.1 5.3 %copy.5 = f32[1024,1024]{0,1:T(8,128)} copy(f32[1024,1024]{1,0:T(8,128)} %param.6) | data formatting | bytes 8388608 | tf_op args[2]
  15.4 30.7 %all-gather.5.cloned.1.call-done = bf16[2048,1024]{1,0:T(8,128)(2,1)} async-done(((bf16[512,1024]{1,0:T(8,128)(2,1)}), bf16[2048,1024]{1,0:T(8,128)(2,1)}) %all-gather.5.cloned.1.call-update) | async-done | bytes 4194320 | tf_op jit(solution)/shard_map/all_gather | solution.py:16
  46.1 76.7 %all-gather.3.cloned.1.call-done = bf16[1024,2048]{1,0:T(8,128)(2,1)} async-done(((bf16[1024,256]{1,0:T(8,128)(2,1)}), bf16[1024,2048]{1,0:T(8,128)(2,1)}) %all-gather.3.cloned.1.call-update) | async-done | bytes 4194320 | tf_op jit(solution)/shard_map/all_gather | solution.py:15
  122.8 11.3 %multiply_reduce_fusion = (f32[1024]{0:T(1024)S(1)}, f32[1024,1024]{0,1:T(8,128)}) fusion(f32[1024,1024]{0,1:T(8,128)} %copy.5, bf16[1024,2048]{1,0:T(8,128)(2,1)} %all-gather.3.cloned.1.call-done, bf16[2048,1024]{1,0:T(8,128)(2,1)} %all-gather.5.cloned.1.call-done), kind=kOutput, calls=%fused_computation | convolution fusion | flops 4298112000 | bytes 16781312 | tf_op jit(solution)/shard_map/dot_general | solution.py:8
  134.1 18.6 %psum.7 = f32[1024]{0:T(1024)S(1)} all-reduce(f32[1024]{0:T(1024)S(1)} %get-tuple-element.5), channel_id=1, replica_groups=mesh['gy'=4,'gx'=8] {'gx'}, use_global_device_ids=true, to_apply=%region_1.0 | all-reduce | flops 1024 | bytes 8192 | tf_op jit(solution)/shard_map/psum | solution.py:18
  152.7 5.0 %broadcast_multiply_fusion = f32[1024,1024]{0,1:T(8,128)} fusion(f32[1024,1024]{0,1:T(8,128)} %get-tuple-element.6, f32[1024]{0:T(1024)S(1)} %add_rsqrt_fusion), kind=kLoop, calls=%fused_computation.1 | loop fusion | flops 1048576 | bytes 8392704 | tf_op jit(solution)/shard_map/mul | solution.py:20
  157.7 5.3 %copy.6 = f32[1024,1024]{1,0:T(8,128)} copy(f32[1024,1024]{0,1:T(8,128)} %broadcast_multiply_fusion) | data formatting | bytes 8388608 | tf_op jit(solution)/shard_map/mul | solution.py:20
  (1 shorter events, 0.0 us)
Async XLA Ops:
  6.5 39.6 %all-gather.5.cloned.1.call-start = ((), (), s32[]{:S(2)}) async-start(), calls=%async_computation.1 | async-start | bytes 5242880 | tf_op jit(solution)/shard_map/all_gather | solution.py:16
  7.3 115.6 %all-gather.3.cloned.1.call-start = ((), (), s32[]{:S(2)}) async-start(), calls=%async_computation | async-start | bytes 4718592 | tf_op jit(solution)/shard_map/all_gather | solution.py:15
Sparse Core Ops, SparseCore 0:
  8.9 37.1 all-gather.4
  48.1 74.6 all-gather.2
where the time goes:
time: 170 us
  waiting for transfers between devices  108 us (64%)
  blocking collectives  18.6 us (11%)
  between operations  13.4 us (8%)
  local copies, waits for them, and re-layouts  11.4 us (7%)
  matrix products  11.3 us (7%)
  other arithmetic  6.98 us (4%)
    all_gather x1, waiting for transfers between devices, shards(): left_line = lax.all_gather(scaled_left, 'gx', axis=1, tiled=True)  76.7 us
    all_gather x1, waiting for transfers between devices, shards(): lax.all_gather(second_factor, 'gy', axis=0, tiled=True)  30.7 us
    psum x1, blocking collectives, shards(): row_power = lax.psum(jnp.sum(corrected * corrected, axis=1), 'gx')  18.6 us
    dot_general x1, matrix products, join_panel(): return jnp.dot(left_panel, right_panel, preferred_element_type=jnp.float32)  11.3 us
    unnamed x1, local copies, waits for them, and re-layouts  5.35 us
    mul x1, local copies, waits for them, and re-layouts, shards(): corrected * lax.rsqrt(row_power / (corrected.shape[1] * lax.axis_size('gx...  5.34 us
    mul x1, other arithmetic, shards(): corrected * lax.rsqrt(row_power / (corrected.shape[1] * lax.axis_size('gx...  4.98 us
  transfers between devices with their start and end apart: 2, of which 2 were waited for; matrix products, arithmetic and copies ran while one was open for 5% of the time, Pallas kernels for 0%

commit v1 on v0

--- a/solution.py
+++ b/solution.py
@@ -15,7 +15,7 @@
     left_line = lax.all_gather(scaled_left, "gx", axis=1, tiled=True)
     total = join_panel(left_line, lax.all_gather(second_factor, "gy", axis=0, tiled=True))
     corrected = result_in - total
-    row_power = lax.psum(jnp.sum(corrected * corrected, axis=1), "gx")
+    row_power = jnp.sum(lax.all_gather(jnp.sum(corrected * corrected, axis=1), "gx"), axis=0)
     corrected = (
         corrected
         * lax.rsqrt(row_power / (corrected.shape[1] * lax.axis_size("gx")) + 1e-06)[:, None]

time: 170 us -> 182 us (1.071)
  blocking collectives: 18.6 us -> 30.6 us
    all_gather x0 -> x1, blocking collectives: none -> 30.6 us  [shards(): lax.all_gather(jnp.sum(corrected * corrected, axis=1), 'gx')]
    psum x1 -> x0, blocking collectives: 18.6 us -> none  [shards(): row_power = lax.psum(jnp.sum(corrected * corrected, axis=1), 'gx')]
  transfers between devices with their start and end apart: 2 -> 2, of which waited for: 2 -> 2; matrix products, arithmetic and copies ran while one was open for 5% -> 4% of each run, Pallas kernels for 0% -> 0%
where the time goes in v1:
time: 182 us
  waiting for transfers between devices  108 us (59%)
  blocking collectives  30.6 us (17%)
  between operations  13.4 us (7%)
  local copies, waits for them, and re-layouts  11.5 us (6%)
  matrix products  11.3 us (6%)
  other arithmetic  6.99 us (4%)
    all_gather x1, waiting for transfers between devices, shards(): left_line = lax.all_gather(scaled_left, 'gx', axis=1, tiled=True)  76.7 us
    all_gather x1, waiting for transfers between devices, shards(): lax.all_gather(second_factor, 'gy', axis=0, tiled=True)  30.7 us
    all_gather x1, blocking collectives, shards(): lax.all_gather(jnp.sum(corrected * corrected, axis=1), 'gx')  30.6 us
    dot_general x1, matrix products, join_panel(): return jnp.dot(left_panel, right_panel, preferred_element_type=jnp.float32)  11.3 us
    unnamed x1, local copies, waits for them, and re-layouts  5.35 us
    mul x1, local copies, waits for them, and re-layouts, shards(): corrected * lax.rsqrt(row_power / (corrected.shape[1] * lax.axis_size('gx...  5.34 us
    mul x1, other arithmetic, shards(): corrected * lax.rsqrt(row_power / (corrected.shape[1] * lax.axis_size('gx...  4.98 us
  transfers between devices with their start and end apart: 2, of which 2 were waited for; matrix products, arithmetic and copies ran while one was open for 4% of the time, Pallas kernels for 0%

profile of v1, /device:TPU:0, one launch (start us, length us, event | category | flops | bytes accessed | tf_op | source)
XLA Modules:
  0.0 181.9 jit_solution(1931856246170519597)
XLA Ops:
  6.5 0.0 all-gather.6.cloned.1.call-start
  6.5 0.7 all-gather.6.cloned.1.call-update
  7.3 0.0 all-gather.4.cloned.1.call-start
  7.3 0.8 dynamic_slice.3
  8.1 2.0 %multiply_convert_fusion = bf16[1024,256]{1,0:T(8,128)(2,1)} fusion(bf16[1024,256]{1,0:T(8,128)(2,1)} %param.4, f32[256]{0:T(256)S(1)} %dynamic_slice.3), kind=kLoop, calls=%fused_computation.3 | loop fusion | flops 786432 | bytes 1049600 | tf_op jit(solution)/shard_map/convert_element_type | solution.py:14
  10.1 0.0 all-gather.4.cloned.1.call-update
  10.1 5.3 %copy.9 = f32[1024,1024]{0,1:T(8,128)} copy(f32[1024,1024]{1,0:T(8,128)} %param.6) | data formatting | bytes 8388608 | tf_op args[2]
  15.4 30.7 %all-gather.6.cloned.1.call-done = bf16[2048,1024]{1,0:T(8,128)(2,1)} async-done(((bf16[512,1024]{1,0:T(8,128)(2,1)}), bf16[2048,1024]{1,0:T(8,128)(2,1)}) %all-gather.6.cloned.1.call-update) | async-done | bytes 4194320 | tf_op jit(solution)/shard_map/all_gather | solution.py:16
  46.1 76.7 %all-gather.4.cloned.1.call-done = bf16[1024,2048]{1,0:T(8,128)(2,1)} async-done(((bf16[1024,256]{1,0:T(8,128)(2,1)}), bf16[1024,2048]{1,0:T(8,128)(2,1)}) %all-gather.4.cloned.1.call-update) | async-done | bytes 4194320 | tf_op jit(solution)/shard_map/all_gather | solution.py:15
  122.8 11.3 %multiply_reduce_fusion = (f32[1024]{0:T(1024)S(1)}, f32[1024,1024]{0,1:T(8,128)}) fusion(f32[1024,1024]{0,1:T(8,128)} %copy.9, bf16[1024,2048]{1,0:T(8,128)(2,1)} %all-gather.4.cloned.1.call-done, bf16[2048,1024]{1,0:T(8,128)(2,1)} %all-gather.6.cloned.1.call-done), kind=kOutput, calls=%fused_computation | convolution fusion | flops 4298112000 | bytes 16781312 | tf_op jit(solution)/shard_map/dot_general | solution.py:8
  134.1 30.6 %all-gather = f32[8192]{0:T(1024)S(1)} all-gather(f32[1024]{0:T(1024)S(1)} %get-tuple-element.5), channel_id=2, replica_groups=mesh['gy'=4,'gx'=8] {'gx'}, dimensions={0}, use_global_device_ids=true | all-gather | bytes 36864 | tf_op jit(solution)/shard_map/all_gather | solution.py:18
  164.8 5.0 %broadcast_multiply_fusion = f32[1024,1024]{0,1:T(8,128)} fusion(f32[1024,1024]{0,1:T(8,128)} %get-tuple-element.6, f32[1024]{0:T(1024)S(1)} %add_rsqrt_fusion), kind=kLoop, calls=%fused_computation.1 | loop fusion | flops 1048576 | bytes 8392704 | tf_op jit(solution)/shard_map/mul | solution.py:20
  169.8 5.3 %copy.10 = f32[1024,1024]{1,0:T(8,128)} copy(f32[1024,1024]{0,1:T(8,128)} %broadcast_multiply_fusion) | data formatting | bytes 8388608 | tf_op jit(solution)/shard_map/mul | solution.py:20
  (3 shorter events, 0.0 us)
Async XLA Ops:
  6.5 39.6 %all-gather.6.cloned.1.call-start = ((), (), s32[]{:S(2)}) async-start(), calls=%async_computation.1 | async-start | bytes 5242880 | tf_op jit(solution)/shard_map/all_gather | solution.py:16
  7.3 115.6 %all-gather.4.cloned.1.call-start = ((), (), s32[]{:S(2)}) async-start(), calls=%async_computation | async-start | bytes 4718592 | tf_op jit(solution)/shard_map/all_gather | solution.py:15
Sparse Core Ops, SparseCore 0:
  8.9 37.1 all-gather.5
  48.1 74.6 all-gather.3
